TPU v7x, 8 devices: a whole 2x2x1 slice. The times are simulated.
8 devices in a mesh: data: 2 (over z, y), tp: 4 (over x, core).
Axes of the slice: x: 2, y: 2, z: 1, core: 2. Of those that a mesh axis runs over, the one named last changes fastest.
Arguments:
- x: bfloat16 [2048, 49152], P('data', 'tp'), parts along dimension 0
- w: bfloat16 [49152, 12288], P('tp')
Outputs:
- output: bfloat16 [2048, 12288], P('data'), parts along dimension 0
There are 2 independent parts. A program takes and returns all parts, laid end to end along the dimension named above; an argument that names none is the same for every part.
All inputs are finite; a program needn't handle non-finite values.
Results may differ from a plain program's by a relative error of at most 0.0103027.
Values are sent between devices in bfloat16 or wider.
A program may use at most 1.5 GiB of HBM per device.

v0:
```python
import jax
import jax.numpy as jnp
from jax import lax
from jax.sharding import PartitionSpec as P, NamedSharding


def solution(mesh):
    def local(x, w):
        partial_y = jnp.dot(x, w, preferred_element_type=jnp.float32).astype(jnp.bfloat16)
        reduced = lax.psum_scatter(partial_y, "tp", scatter_dimension=0, tiled=True)
        return lax.all_gather(reduced, "tp", axis=0, tiled=True)

    return jax.shard_map(local, mesh=mesh, in_specs=(P("data", "tp"), P("tp", None)), out_specs=P("data", None), check_vma=False)
```

profile of v0, /device:TPU:0, one launch (start us, length us, event | category | flops | bytes accessed | tf_op | source)
XLA Modules:
  0.0 688.5 jit_solution(14369435314914029034)
XLA Ops:
  6.5 0.0 reduce-scatter.2.cloned.1.call-start
  6.5 327.7 %convolution_convert_fusion = bf16[1024,12288]{1,0:T(8,128)(2,1)} fusion(bf16[1024,12288]{1,0:T(8,128)(2,1)} %param.2, bf16[12288,12288]{1,0:T(8,128)(2,1)} %param.3), kind=kOutput, calls=%fused_computation | convolution fusion | flops 309250228224 | bytes 352321536 | tf_op jit(solution)/shard_map/dot_general | solution.py:9
  334.2 0.0 reduce-scatter.2.cloned.1.call-update
  334.3 0.0 all-gather.2.cloned.1.call-start
  334.3 172.0 %reduce-scatter.2.cloned.1.call-done = bf16[256,12288]{1,0:T(8,128)(2,1)} async-done(((bf16[1024,12288]{1,0:T(8,128)(2,1)}), bf16[256,12288]{1,0:T(8,128)(2,1)}) %reduce-scatter.2.cloned.1.call-update) | async-done | bytes 6291472 | tf_op jit(solution)/shard_map/reduce_scatter | solution.py:10
  506.3 0.0 all-gather.2.cloned.1.call-update
  506.4 154.4 %all-gather.2.cloned.1.call-done = bf16[1024,12288]{1,0:T(8,128)(2,1)} async-done(((bf16[256,12288]{1,0:T(8,128)(2,1)}), bf16[1024,12288]{1,0:T(8,128)(2,1)}) %all-gather.2.cloned.1.call-update) | async-done | bytes 25165840 | tf_op jit(solution)/shard_map/all_gather | solution.py:11
  660.8 20.9 %copy.4 = bf16[1024,12288]{1,0:T(8,128)(2,1)} copy(bf16[1024,12288]{1,0:T(8,128)(2,1)} %all-gather.2.cloned.1.call-done) | data formatting | bytes 50331648
Async XLA Ops:
  6.5 499.8 %reduce-scatter.2.cloned.1.call-start = ((), (), s32[]{:S(2)}) async-start(), calls=%async_computation.1 | async-start | bytes 31457280 | tf_op jit(solution)/shard_map/reduce_scatter | solution.py:10
  334.3 326.5 %all-gather.2.cloned.1.call-start = ((), (), s32[]{:S(2)}) async-start(), calls=%async_computation.2 | async-start | bytes 31457280 | tf_op jit(solution)/shard_map/all_gather | solution.py:11
Sparse Core Ops, SparseCore 0:
  334.4 171.8 reduce-scatter.1
  507.9 152.8 all-gather.1
where the time goes:
time: 689 us; the launch traced here: 688 us
  matrix products  328 us (48%)
  waiting for transfers between devices  326 us (47%)
  local copies, waits for them, and re-layouts  20.9 us (3%)
  between operations  13.4 us (2%)
    dot_general x1, matrix products, local(): jnp.dot(x, w, preferred_element_type=jnp.float32).astype(jnp.bfloat16)  328 us
    reduce_scatter x1, waiting for transfers between devices, local(): reduced = lax.psum_scatter(partial_y, 'tp', scatter_dimension=0, tiled=True)  172 us
    all_gather x1, waiting for transfers between devices, local(): return lax.all_gather(reduced, 'tp', axis=0, tiled=True)  154 us
    unnamed x1, local copies, waits for them, and re-layouts  20.9 us
  transfers between devices with their start and end apart: 2, of which 2 were waited for; matrix products, arithmetic and copies ran while one was open for 0% of the time, Pallas kernels for 0%

commit v1 on v0

v1 whole, which is shorter than its diff:
```python
import functools

import jax
import jax.numpy as jnp
from jax import lax
from jax.experimental import pallas as pl
from jax.experimental.pallas import tpu as pltpu
from jax.sharding import PartitionSpec as P

BF16, F32 = jnp.bfloat16, jnp.float32
NC = 512
BK = 2048
HR = 256
SLOTS = 6


def kernel(nb, nch, x_hbm, w_hbm, r_hbm, xv, wv, part, sb1, rb1, ch, rb2, yb,
           xsem, wsem, s1s, s1r, s2s, s2r, s4s, s4r, lsem):
    me = lax.axis_index("tp")
    core = lax.rem(me, 2)
    partner = me + 1 - 2 * core
    across = lax.rem(me + 2, 4)
    off = (pl.multiple_of((1 - core) * HR, HR),
           pl.multiple_of(core * HR, HR))

    def x_copy(p, h, b):
        row = pl.multiple_of(p * 2 * HR + off[h], HR)
        return pltpu.make_async_copy(
            x_hbm.at[pl.ds(row, HR), pl.ds(b * BK, BK)],
            xv.at[p, pl.ds(off[h], HR), pl.ds(b * BK, BK)], xsem.at[2 * p + h, b])

    def w_copy(n, b):
        col = pl.multiple_of(n * NC, NC)
        par = lax.rem(n, 2)
        return pltpu.make_async_copy(
            w_hbm.at[pl.ds(b * BK, BK), pl.ds(col, NC)],
            wv.at[par, pl.ds(b * BK, BK), :], wsem.at[par, b])

    def remote(src, dst, ssem, rsem, to):
        return pltpu.make_async_remote_copy(
            src_ref=src, dst_ref=dst, send_sem=ssem, recv_sem=rsem,
            device_id={"tp": to}, device_id_type=pl.DeviceIdType.MESH)

    def send1(u):
        p, s = lax.rem(u, 2), lax.rem(u, 4)
        return remote(sb1.at[p], rb1.at[s], s1s.at[p], s1r.at[s], partner)

    def send2(u):
        s = lax.rem(u, SLOTS)
        return remote(ch.at[s], rb2.at[s], s2s.at[s], s2r.at[s], across)

    def place(u):
        row = lax.rem(u, 2) * 2 * HR + core * HR
        return r_hbm.at[pl.ds(pl.multiple_of(row, HR), HR), pl.ds(pl.multiple_of(u // 2 * NC, NC), NC)]

    def send4(u, s):
        return remote(yb.at[s], place(u), s4s.at[s], s4r.at[lax.rem(u, 4)], partner)

    def keep4(u, s):
        return pltpu.make_async_copy(yb.at[s], place(u), lsem.at[s])

    def done(copy):
        copy.wait_recv()
        copy.wait_send()

    def start4(u, s):
        send4(u, s).start()
        keep4(u, s).start()

    def wait4(u, s):
        done(send4(u, s))
        keep4(u, s).wait()

    def dot(n, p, h, k0=0, k1=nb):
        return jnp.dot(xv[p, pl.ds(off[h], HR), pl.ds(k0 * BK, (k1 - k0) * BK)],
                       wv[lax.rem(n, 2), pl.ds(k0 * BK, (k1 - k0) * BK), :], preferred_element_type=F32)

    def theirs(n, p):
        sb1[p] = dot(n, p, 0).astype(BF16)

    def ours(n, p):
        u = 2 * n + p
        ch[lax.rem(u, SLOTS)] = (dot(n, p, 1) + rb1[lax.rem(u, 4)].astype(F32)).astype(BF16)

    def add2(u, s):
        slot = lax.rem(u + SLOTS, SLOTS)
        yb[s] = ch[slot] + rb2[slot]

    for b in range(nb):
        x_copy(0, 0, b).start()
        w_copy(0, b).start()
        x_copy(1, 0, b).start()
    for p in range(2):
        for b in range(nb):
            x_copy(p, 1, b).start()
    for b in range(nb):
        w_copy(1, b).start()

    barrier = pltpu.get_barrier_semaphore()
    for other in (partner, across):
        pl.semaphore_signal(barrier, inc=1, device_id={"tp": other},
                            device_id_type=pl.DeviceIdType.MESH)
    pl.semaphore_wait(barrier, 2)

    for b in range(nb):
        x_copy(0, 0, b).wait()
        w_copy(0, b).wait()
        x_copy(1, 0, b).wait()
        for p in range(2):
            d = dot(0, p, 0, b, b + 1)
            if b == 0:
                part[p] = d
            elif b < nb - 1:
                part[p] += d
            else:
                sb1[p] = (part[p] + d).astype(BF16)
    send1(0).start()

    @pl.loop(0, nch - 1)
    def _(n):
        u = 2 * n
        done(send1(u))
        send1(u + 1).start()

        @pl.when(n >= 2)
        def _():
            start4(u - 3, 1)

        @pl.when(n == 0)
        def _():
            for b in range(nb):
                x_copy(0, 1, b).wait()
        ours(n, 0)

        @pl.when(n >= 1)
        def _():
            done(send2(u - 2))
        send2(u).start()

        @pl.when(n >= 2)
        def _():
            wait4(u - 3, 1)
        for b in range(nb):
            w_copy(n + 1, b).wait()
        theirs(n + 1, 0)
        add2(u - 2, 0)

        done(send1(u + 1))
        send1(u + 2).start()

        @pl.when(n >= 1)
        def _():
            start4(u - 2, 0)

        @pl.when(n == 0)
        def _():
            for b in range(nb):
                x_copy(1, 1, b).wait()
        ours(n, 1)

        @pl.when(n >= 1)
        def _():
            done(send2(u - 1))
        send2(u + 1).start()

        @pl.when(n >= 1)
        def _():
            wait4(u - 2, 0)

        @pl.when(n < nch - 2)
        def _():
            for b in range(nb):
                w_copy(n + 2, b).start()
        theirs(n + 1, 1)
        add2(u - 1, 1)

    n, u = nch - 1, 2 * nch - 2
    done(send1(u))
    send1(u + 1).start()
    start4(u - 3, 1)
    ours(n, 0)
    done(send2(u - 2))
    send2(u).start()
    wait4(u - 3, 1)
    done(send1(u + 1))
    ours(n, 1)
    send2(u + 1).start()
    add2(u - 2, 0)
    start4(u - 2, 0)
    done(send2(u - 1))
    add2(u - 1, 1)
    start4(u - 1, 1)
    for v in (u, u + 1):
        s = v % 2
        wait4(v - 2, s)
        done(send2(v))
        add2(v, s)
        start4(v, s)
    for v in (u, u + 1):
        wait4(v, v % 2)


def solution(mesh):
    def local(x, w):
        rows, depth = x.shape
        cols = w.shape[1]
        nb, nch = depth // BK, cols // NC
        dma = pltpu.SemaphoreType.DMA
        return pl.pallas_call(
            functools.partial(kernel, nb, nch),
            out_shape=jax.ShapeDtypeStruct((rows, cols), BF16),
            in_specs=[pl.BlockSpec(memory_space=pl.ANY)] * 2,
            out_specs=pl.BlockSpec(memory_space=pl.ANY),
            scratch_shapes=[
                pltpu.VMEM((2, 2 * HR, depth), BF16),
                pltpu.VMEM((2, depth, NC), BF16),
                pltpu.VMEM((2, HR, NC), F32),
                pltpu.VMEM((2, HR, NC), BF16),
                pltpu.VMEM((4, HR, NC), BF16),
                pltpu.VMEM((SLOTS, HR, NC), BF16),
                pltpu.VMEM((SLOTS, HR, NC), BF16),
                pltpu.VMEM((2, HR, NC), BF16),
                dma((4, nb)), dma((2, nb)),
                dma((2,)), dma((4,)),
                dma((SLOTS,)), dma((SLOTS,)),
                dma((2,)), dma((4,)), dma((2,)),
            ],
            compiler_params=pltpu.CompilerParams(
                collective_id=0, has_side_effects=True, vmem_limit_bytes=63 * 1024 * 1024),
            cost_estimate=pl.CostEstimate(
                flops=2 * rows * depth * cols, transcendentals=0,
                bytes_accessed=2 * (rows * depth + depth * cols + rows * cols)),
            name="rowparallel",
        )(x, w)

    return jax.shard_map(local, mesh=mesh, in_specs=(P("data", "tp"), P("tp", None)),
                         out_specs=P("data", None), check_vma=False)
```

time: 689 us -> 371 us (0.54)
  Pallas kernels: 0 us -> 350 us
  matrix products: 328 us -> 0 us
  waiting for transfers between devices: 326 us -> 0 us
  between operations: 13.4 us -> 0.01 us
    pallas_call x0 -> x1, Pallas kernels: none -> 350 us  [local(): pl.pallas_call(functools.partial(kernel, nb, nch), out_shape=jax.ShapeDty...]
    dot_general x1 -> x0, matrix products: 328 us -> none  [local(): jnp.dot(x, w, preferred_element_type=jnp.float32).astype(jnp.bfloat16)]
    reduce_scatter x1 -> x0, waiting for transfers between devices: 172 us -> none  [local(): reduced = lax.psum_scatter(partial_y, 'tp', scatter_dimension=0, tiled=True)]
    all_gather x1 -> x0, waiting for transfers between devices: 154 us -> none  [local(): return lax.all_gather(reduced, 'tp', axis=0, tiled=True)]
  transfers between devices with their start and end apart: 2 -> 0, of which waited for: 2 -> 0; matrix products, arithmetic and copies ran while one was open for 0% -> 0% of each run, Pallas kernels for 0% -> 0%
where the time goes in v1:
time: 371 us
  Pallas kernels  350 us (94%)
  local copies, waits for them, and re-layouts  20.9 us (6%)
    pallas_call x1, Pallas kernels, local(): pl.pallas_call(functools.partial(kernel, nb, nch), out_shape=jax.ShapeDty...  350 us
    unnamed x1, local copies, waits for them, and re-layouts  20.9 us

profile of v1, /device:TPU:0, one launch (start us, length us, event | category | flops | bytes accessed | tf_op | source)
XLA Modules:
  0.0 371.2 jit_solution(9172486571378660221)
XLA Ops:
  0.0 350.3 %rowparallel.1 = bf16[1024,12288]{1,0:T(8,128)(2,1)} custom-call(bf16[1024,12288]{1,0:T(8,128)(2,1)} %x_hbm.1, bf16[12288,12288]{1,0:T(8,128)(2,1)} %w_hbm.1), custom_call_target="tpu_custom_call" | custom-call | flops 309237645312 | bytes 352321536 | tf_op jit(solution)/shard_map/rowparallel/pallas_call | solution.py:209
  350.3 20.9 %copy.4 = bf16[1024,12288]{1,0:T(8,128)(2,1)} copy(bf16[1024,12288]{1,0:T(8,128)(2,1)} %rowparallel.1) | data formatting | bytes 50331648

commit v2 on v0

v2 whole, which is shorter than its diff:
```python
import functools

import jax
import jax.numpy as jnp
from jax import lax
from jax.experimental import pallas as pl
from jax.experimental.pallas import tpu as pltpu
from jax.sharding import PartitionSpec as P

BF16, F32 = jnp.bfloat16, jnp.float32
NC = 256
BK = 2048
WS = 4
SLOTS = 6


def kernel(nb, nu, hr, x_hbm, w_hbm, r_hbm, xv, wv, part, sb1, rb1, ch, rb2, yb,
           xsem, wsem, s1s, s1r, s2s, s2r, s4s, s4r, lsem):
    me = lax.axis_index("tp")
    core = lax.rem(me, 2)
    partner = me + 1 - 2 * core
    across = lax.rem(me + 2, 4)
    off_o = pl.multiple_of((1 - core) * hr, hr)
    off_m = pl.multiple_of(core * hr, hr)

    def x_copy(b):
        return pltpu.make_async_copy(
            x_hbm.at[:, pl.ds(b * BK, BK)], xv.at[:, pl.ds(b * BK, BK)], xsem.at[b])

    def w_copy(u, b):
        col = pl.multiple_of(u * NC, NC)
        s = lax.rem(u, WS)
        return pltpu.make_async_copy(
            w_hbm.at[pl.ds(b * BK, BK), pl.ds(col, NC)],
            wv.at[s, pl.ds(b * BK, BK), :], wsem.at[s, b])

    def remote(src, dst, ssem, rsem, to):
        return pltpu.make_async_remote_copy(
            src_ref=src, dst_ref=dst, send_sem=ssem, recv_sem=rsem,
            device_id={"tp": to}, device_id_type=pl.DeviceIdType.MESH)

    def send1(u):
        p, s = lax.rem(u, 2), lax.rem(u, 4)
        return remote(sb1.at[p], rb1.at[s], s1s.at[p], s1r.at[s], partner)

    def send2(u):
        s = lax.rem(u, SLOTS)
        return remote(ch.at[s], rb2.at[s], s2s.at[s], s2r.at[s], across)

    def place(u):
        return r_hbm.at[pl.ds(off_m, hr), pl.ds(pl.multiple_of(u * NC, NC), NC)]

    def send4(u):
        p = lax.rem(u, 2)
        return remote(yb.at[p], place(u), s4s.at[p], s4r.at[lax.rem(u, 4)], partner)

    def keep4(u):
        p = lax.rem(u, 2)
        return pltpu.make_async_copy(yb.at[p], place(u), lsem.at[p])

    def done(copy):
        copy.wait_recv()
        copy.wait_send()

    def start4(u):
        send4(u).start()
        keep4(u).start()

    def wait4(u):
        done(send4(u))
        keep4(u).wait()

    def theirs(u, cuts=1):
        r = hr // cuts
        for c in range(cuts):
            sb1[lax.rem(u, 2), pl.ds(c * r, r), :] = jnp.dot(
                xv[pl.ds(off_o + c * r, r), :], wv[lax.rem(u, WS)], preferred_element_type=F32).astype(BF16)

    def ours(u, cuts=1):
        r = hr // cuts
        for c in range(cuts):
            ch[lax.rem(u, SLOTS), pl.ds(c * r, r), :] = (
                jnp.dot(xv[pl.ds(off_m + c * r, r), :], wv[lax.rem(u, WS)], preferred_element_type=F32)
                + rb1[lax.rem(u, 4), pl.ds(c * r, r), :].astype(F32)).astype(BF16)

    def add2(u):
        slot = lax.rem(u + SLOTS, SLOTS)
        yb[lax.rem(u + 2, 2)] = ch[slot] + rb2[slot]

    for b in range(nb):
        x_copy(b).start()
        w_copy(0, b).start()
        w_copy(1, b).start()
    for u in (2, 3):
        for b in range(nb):
            w_copy(u, b).start()

    barrier = pltpu.get_barrier_semaphore()
    for other in (partner, across):
        pl.semaphore_signal(barrier, inc=1, device_id={"tp": other},
                            device_id_type=pl.DeviceIdType.MESH)
    pl.semaphore_wait(barrier, 2)

    for b in range(nb):
        x_copy(b).wait()
        w_copy(0, b).wait()
        w_copy(1, b).wait()
        for u in range(2):
            d = jnp.dot(xv[:, pl.ds(b * BK, BK)], wv[u, pl.ds(b * BK, BK), :], preferred_element_type=F32)
            if b == 0:
                part[u] = d
            else:
                part[u] += d
    for u in range(2):
        sb1[u] = part[u, pl.ds(off_o, hr), :].astype(BF16)
    send1(0).start()
    send1(1).start()
    for b in range(nb):
        w_copy(4, b).start()
        w_copy(2, b).wait()
    done(send1(0))
    theirs(2, 2)
    done(send1(1))
    send1(2).start()
    for b in range(nb):
        w_copy(3, b).wait()
    theirs(3, 2)
    for u in range(2):
        ch[u] = (part[u, pl.ds(off_m, hr), :] + rb1[u].astype(F32)).astype(BF16)
    send2(0).start()

    @pl.loop(2, nu - 2)
    def _(u):
        done(send1(u))

        @pl.when(u >= 3)
        def _():
            done(send2(u - 3))

        @pl.when(u >= 5)
        def _():
            wait4(u - 5)
        send1(u + 1).start()
        send2(u - 1).start()

        @pl.when(u >= 4)
        def _():
            start4(u - 4)

        @pl.when(u < nu - 3)
        def _():
            for b in range(nb):
                w_copy(u + 3, b).start()
        for b in range(nb):
            w_copy(u + 2, b).wait()
        ours(u)
        theirs(u + 2)
        add2(u - 3)

    for u in (nu - 2, nu - 1):
        done(send1(u))
        done(send2(u - 3))
        wait4(u - 5)
        if u + 1 < nu:
            send1(u + 1).start()
        send2(u - 1).start()
        start4(u - 4)
        ours(u, 2)
        add2(u - 3)
    send2(nu - 1).start()
    start4(nu - 4)
    for u in range(nu - 3, nu):
        done(send2(u))
        wait4(u - 2)
        add2(u)
        start4(u)
    wait4(nu - 2)
    wait4(nu - 1)


CP = 32


def last_copy(r_hbm, y_hbm, buf, isem, osem):
    n = buf.shape[0]

    def into(i):
        return pltpu.make_async_copy(r_hbm.at[pl.ds(i * CP, CP), :], buf.at[i], isem.at[i])

    def out(i):
        return pltpu.make_async_copy(buf.at[i], y_hbm.at[pl.ds(i * CP, CP), :], osem.at[i])

    for i in range(n):
        into(i).start()
    for i in range(n):
        into(i).wait()
        out(i).start()
    for i in range(n):
        out(i).wait()


def solution(mesh):
    def local(x, w):
        rows, depth = x.shape
        cols = w.shape[1]
        nb, nu, hr = depth // BK, cols // NC, rows // 2
        dma = pltpu.SemaphoreType.DMA
        r = pl.pallas_call(
            functools.partial(kernel, nb, nu, hr),
            out_shape=jax.ShapeDtypeStruct((rows, cols), BF16),
            in_specs=[pl.BlockSpec(memory_space=pl.ANY)] * 2,
            out_specs=pl.BlockSpec(memory_space=pl.ANY),
            scratch_shapes=[
                pltpu.VMEM((rows, depth), BF16),
                pltpu.VMEM((WS, depth, NC), BF16),
                pltpu.VMEM((2, rows, NC), F32),
                pltpu.VMEM((2, hr, NC), BF16),
                pltpu.VMEM((4, hr, NC), BF16),
                pltpu.VMEM((SLOTS, hr, NC), BF16),
                pltpu.VMEM((SLOTS, hr, NC), BF16),
                pltpu.VMEM((2, hr, NC), BF16),
                dma((nb,)), dma((WS, nb)),
                dma((2,)), dma((4,)),
                dma((SLOTS,)), dma((SLOTS,)),
                dma((2,)), dma((4,)), dma((2,)),
            ],
            compiler_params=pltpu.CompilerParams(
                collective_id=0, has_side_effects=True, vmem_limit_bytes=63 * 1024 * 1024),
            cost_estimate=pl.CostEstimate(
                flops=2 * rows * depth * cols, transcendentals=0,
                bytes_accessed=2 * (rows * depth + depth * cols + rows * cols)),
            name="rowparallel",
        )(x, w)

        return pl.pallas_call(
            last_copy,
            out_shape=jax.ShapeDtypeStruct((rows, cols), BF16),
            in_specs=[pl.BlockSpec(memory_space=pl.ANY)],
            out_specs=pl.BlockSpec(memory_space=pl.ANY),
            scratch_shapes=[pltpu.VMEM((rows // CP, CP, cols), BF16), dma((rows // CP,)), dma((rows // CP,))],
            compiler_params=pltpu.CompilerParams(vmem_limit_bytes=63 * 1024 * 1024),
            name="lastcopy",
        )(r)

    return jax.shard_map(local, mesh=mesh, in_specs=(P("data", "tp"), P("tp", None)),
                         out_specs=P("data", None), check_vma=False)
```

time: 689 us -> 367 us (0.53)
  Pallas kernels: 0 us -> 367 us
  matrix products: 328 us -> 0 us
  waiting for transfers between devices: 326 us -> 0 us
  local copies, waits for them, and re-layouts: 20.9 us -> 0 us
  between operations: 13.4 us -> 0.17 us
    pallas_call x0 -> x2, Pallas kernels: none -> 367 us  [the longest x1 350 us: local(): pl.pallas_call(functools.partial(kernel, nb, nu, hr), out_shape=jax.Shape...]
    dot_general x1 -> x0, matrix products: 328 us -> none  [local(): jnp.dot(x, w, preferred_element_type=jnp.float32).astype(jnp.bfloat16)]
    reduce_scatter x1 -> x0, waiting for transfers between devices: 172 us -> none  [local(): reduced = lax.psum_scatter(partial_y, 'tp', scatter_dimension=0, tiled=True)]
    all_gather x1 -> x0, waiting for transfers between devices: 154 us -> none  [local(): return lax.all_gather(reduced, 'tp', axis=0, tiled=True)]
    unnamed x1 -> x0, local copies, waits for them, and re-layouts: 20.9 us -> none
  transfers between devices with their start and end apart: 2 -> 0, of which waited for: 2 -> 0; matrix products, arithmetic and copies ran while one was open for 0% -> 0% of each run, Pallas kernels for 0% -> 0%
where the time goes in v2:
time: 367 us
  Pallas kernels  367 us (100%)
    pallas_call x1, Pallas kernels, local(): pl.pallas_call(functools.partial(kernel, nb, nu, hr), out_shape=jax.Shape...  350 us
    pallas_call x1, Pallas kernels, local(): pl.pallas_call(last_copy, out_shape=jax.ShapeDtypeStruct((rows, cols), BF...  17.3 us

profile of v2, /device:TPU:0, one launch (start us, length us, event | category | flops | bytes accessed | tf_op | source)
XLA Modules:
  0.0 367.1 jit_solution(11273595414776281829)
XLA Ops:
  0.0 349.6 %rowparallel.1.r_hbm = bf16[1024,12288]{1,0:T(8,128)(2,1)} custom-call(bf16[1024,12288]{1,0:T(8,128)(2,1)} %x_hbm.1, bf16[12288,12288]{1,0:T(8,128)(2,1)} %w_hbm.1), custom_call_target="tpu_custom_call" | custom-call | flops 309237645312 | bytes 352321536 | tf_op jit(solution)/shard_map/rowparallel/pallas_call | solution.py:208
  349.6 17.3 %lastcopy.1 = bf16[1024,12288]{1,0:T(8,128)(2,1)} custom-call(bf16[1024,12288]{1,0:T(8,128)(2,1)} %rowparallel.1.r_hbm), custom_call_target="tpu_custom_call" | custom-call | tf_op jit(solution)/shard_map/lastcopy/pallas_call | solution.py:235

commit v3 on v2

--- a/solution.py
+++ b/solution.py
@@ -15,7 +15,7 @@
 
 
 def kernel(nb, nu, hr, x_hbm, w_hbm, r_hbm, xv, wv, part, sb1, rb1, ch, rb2, yb,
-           xsem, wsem, s1s, s1r, s2s, s2r, s4s, s4r, lsem):
+           xsem, wsem, wusem, s1s, s1r, s2s, s2r, s4s, s4r, lsem):
     me = lax.axis_index("tp")
     core = lax.rem(me, 2)
     partner = me + 1 - 2 * core
@@ -34,6 +34,11 @@
             w_hbm.at[pl.ds(b * BK, BK), pl.ds(col, NC)],
             wv.at[s, pl.ds(b * BK, BK), :], wsem.at[s, b])
 
+    def w_unit(u):
+        s = lax.rem(u, WS)
+        return pltpu.make_async_copy(
+            w_hbm.at[:, pl.ds(pl.multiple_of(u * NC, NC), NC)], wv.at[s], wusem.at[s])
+
     def remote(src, dst, ssem, rsem, to):
         return pltpu.make_async_remote_copy(
             src_ref=src, dst_ref=dst, send_sem=ssem, recv_sem=rsem,
@@ -52,7 +57,7 @@
 
     def send4(u):
         p = lax.rem(u, 2)
-        return remote(yb.at[p], place(u), s4s.at[p], s4r.at[lax.rem(u, 4)], partner)
+        return remote(yb.at[p], place(u), s4s.at[p], s4r, partner)
 
     def keep4(u):
         p = lax.rem(u, 2)
@@ -67,7 +72,7 @@
         keep4(u).start()
 
     def wait4(u):
-        done(send4(u))
+        send4(u).wait_send()
         keep4(u).wait()
 
     def theirs(u, cuts=1):
@@ -92,8 +97,7 @@
         w_copy(0, b).start()
         w_copy(1, b).start()
     for u in (2, 3):
-        for b in range(nb):
-            w_copy(u, b).start()
+        w_unit(u).start()
 
     barrier = pltpu.get_barrier_semaphore()
     for other in (partner, across):
@@ -115,15 +119,13 @@
         sb1[u] = part[u, pl.ds(off_o, hr), :].astype(BF16)
     send1(0).start()
     send1(1).start()
-    for b in range(nb):
-        w_copy(4, b).start()
-        w_copy(2, b).wait()
+    w_unit(4).start()
+    w_unit(2).wait()
     done(send1(0))
     theirs(2, 2)
     done(send1(1))
     send1(2).start()
-    for b in range(nb):
-        w_copy(3, b).wait()
+    w_unit(3).wait()
     theirs(3, 2)
     for u in range(2):
         ch[u] = (part[u, pl.ds(off_m, hr), :] + rb1[u].astype(F32)).astype(BF16)
@@ -149,10 +151,8 @@
 
         @pl.when(u < nu - 3)
         def _():
-            for b in range(nb):
-                w_copy(u + 3, b).start()
-        for b in range(nb):
-            w_copy(u + 2, b).wait()
+            w_unit(u + 3).start()
+        w_unit(u + 2).wait()
         ours(u)
         theirs(u + 2)
         add2(u - 3)
@@ -176,6 +176,8 @@
         start4(u)
     wait4(nu - 2)
     wait4(nu - 1)
+    theirs_here = r_hbm.at[pl.ds(off_o, hr), :]
+    pltpu.make_async_copy(theirs_here, theirs_here, s4r).wait()
 
 
 CP = 32
@@ -219,10 +221,10 @@
                 pltpu.VMEM((SLOTS, hr, NC), BF16),
                 pltpu.VMEM((SLOTS, hr, NC), BF16),
                 pltpu.VMEM((2, hr, NC), BF16),
-                dma((nb,)), dma((WS, nb)),
+                dma((nb,)), dma((2, nb)), dma((WS,)),
                 dma((2,)), dma((4,)),
                 dma((SLOTS,)), dma((SLOTS,)),
-                dma((2,)), dma((4,)), dma((2,)),
+                dma((2,)), dma(()), dma((2,)),
             ],
             compiler_params=pltpu.CompilerParams(
                 collective_id=0, has_side_effects=True, vmem_limit_bytes=63 * 1024 * 1024),

time: 367 us -> 363 us (0.989)
  Pallas kernels: 367 us -> 363 us
    pallas_call x1, Pallas kernels: 350 us -> 345 us  [local(): pl.pallas_call(functools.partial(kernel, nb, nu, hr), out_shape=jax.Shape...]
where the time goes in v3:
time: 363 us
  Pallas kernels  363 us (100%)
    pallas_call x1, Pallas kernels, local(): pl.pallas_call(functools.partial(kernel, nb, nu, hr), out_shape=jax.Shape...  345 us
    pallas_call x1, Pallas kernels, local(): pl.pallas_call(last_copy, out_shape=jax.ShapeDtypeStruct((rows, cols), BF...  17.3 us

profile of v3, /device:TPU:0, one launch (start us, length us, event | category | flops | bytes accessed | tf_op | source)
XLA Modules:
  0.0 362.9 jit_solution(9086129971186267624)
XLA Ops:
  0.0 345.4 %rowparallel.1.r_hbm = bf16[1024,12288]{1,0:T(8,128)(2,1)} custom-call(bf16[1024,12288]{1,0:T(8,128)(2,1)} %x_hbm.1, bf16[12288,12288]{1,0:T(8,128)(2,1)} %w_hbm.1), custom_call_target="tpu_custom_call" | custom-call | flops 309237645312 | bytes 352321536 | tf_op jit(solution)/shard_map/rowparallel/pallas_call | solution.py:210
  345.4 17.3 %lastcopy.1 = bf16[1024,12288]{1,0:T(8,128)(2,1)} custom-call(bf16[1024,12288]{1,0:T(8,128)(2,1)} %rowparallel.1.r_hbm), custom_call_target="tpu_custom_call" | custom-call | tf_op jit(solution)/shard_map/lastcopy/pallas_call | solution.py:237

commit v4 on v3

--- a/solution.py
+++ b/solution.py
@@ -14,8 +14,8 @@
 SLOTS = 6
 
 
-def kernel(nb, nu, hr, x_hbm, w_hbm, r_hbm, xv, wv, part, sb1, rb1, ch, rb2, yb,
-           xsem, wsem, wusem, s1s, s1r, s2s, s2r, s4s, s4r, lsem):
+def kernel(nb, nu, hr, x_hbm, w_hbm, r_hbm, c_hbm, xv, wv, part, sb1, rb1, ch, rb2, yb,
+           xsem, wsem, wusem, s1s, s1r, s2s, s2r, s4s, s4r, lsem, csem):
     me = lax.axis_index("tp")
     core = lax.rem(me, 2)
     partner = me + 1 - 2 * core
@@ -45,8 +45,8 @@
             device_id={"tp": to}, device_id_type=pl.DeviceIdType.MESH)
 
     def send1(u):
-        p, s = lax.rem(u, 2), lax.rem(u, 4)
-        return remote(sb1.at[p], rb1.at[s], s1s.at[p], s1r.at[s], partner)
+        s = lax.rem(u, 4)
+        return remote(sb1.at[s], rb1.at[s], s1s.at[s], s1r.at[s], partner)
 
     def send2(u):
         s = lax.rem(u, SLOTS)
@@ -63,6 +63,10 @@
         p = lax.rem(u, 2)
         return pltpu.make_async_copy(yb.at[p], place(u), lsem.at[p])
 
+    def keepc(i):
+        return pltpu.make_async_copy(
+            ch.at[(nu - 2 + i) % SLOTS], c_hbm.at[:, pl.ds(i * NC, NC)], csem.at[i])
+
     def done(copy):
         copy.wait_recv()
         copy.wait_send()
@@ -78,7 +82,7 @@
     def theirs(u, cuts=1):
         r = hr // cuts
         for c in range(cuts):
-            sb1[lax.rem(u, 2), pl.ds(c * r, r), :] = jnp.dot(
+            sb1[lax.rem(u, 4), pl.ds(c * r, r), :] = jnp.dot(
                 xv[pl.ds(off_o + c * r, r), :], wv[lax.rem(u, WS)], preferred_element_type=F32).astype(BF16)
 
     def ours(u, cuts=1):
@@ -121,11 +125,11 @@
     send1(1).start()
     w_unit(4).start()
     w_unit(2).wait()
-    done(send1(0))
     theirs(2, 2)
-    done(send1(1))
     send1(2).start()
     w_unit(3).wait()
+    done(send1(0))
+    done(send1(1))
     theirs(3, 2)
     for u in range(2):
         ch[u] = (part[u, pl.ds(off_m, hr), :] + rb1[u].astype(F32)).astype(BF16)
@@ -161,36 +165,39 @@
         done(send1(u))
         done(send2(u - 3))
         wait4(u - 5)
-        if u + 1 < nu:
+        if u == nu - 2:
             send1(u + 1).start()
-        send2(u - 1).start()
+            send2(u - 1).start()
+        else:
+            keepc(0).start()
         start4(u - 4)
         ours(u, 2)
         add2(u - 3)
-    send2(nu - 1).start()
+    keepc(1).start()
     start4(nu - 4)
-    for u in range(nu - 3, nu):
-        done(send2(u))
-        wait4(u - 2)
-        add2(u)
-        start4(u)
-    wait4(nu - 2)
-    wait4(nu - 1)
-    theirs_here = r_hbm.at[pl.ds(off_o, hr), :]
+    done(send2(nu - 3))
+    wait4(nu - 5)
+    add2(nu - 3)
+    start4(nu - 3)
+    wait4(nu - 4)
+    wait4(nu - 3)
+    keepc(0).wait()
+    keepc(1).wait()
+    theirs_here = r_hbm.at[pl.ds(off_o, hr), pl.ds(0, (nu - 2) * NC)]
     pltpu.make_async_copy(theirs_here, theirs_here, s4r).wait()
 
 
 CP = 32
 
 
-def last_copy(r_hbm, y_hbm, buf, isem, osem):
+def last_copy(cols, r_hbm, y_hbm, buf, isem, osem):
     n = buf.shape[0]
 
     def into(i):
-        return pltpu.make_async_copy(r_hbm.at[pl.ds(i * CP, CP), :], buf.at[i], isem.at[i])
+        return pltpu.make_async_copy(r_hbm.at[pl.ds(i * CP, CP), pl.ds(0, cols)], buf.at[i], isem.at[i])
 
     def out(i):
-        return pltpu.make_async_copy(buf.at[i], y_hbm.at[pl.ds(i * CP, CP), :], osem.at[i])
+        return pltpu.make_async_copy(buf.at[i], y_hbm.at[pl.ds(i * CP, CP), pl.ds(0, cols)], osem.at[i])
 
     for i in range(n):
         into(i).start()
@@ -201,30 +208,43 @@
         out(i).wait()
 
 
+def last_units(y_in, mine, other, y_hbm, sem):
+    core = lax.rem(lax.axis_index("tp"), 2)
+    hr, width = mine.shape
+    first = y_hbm.shape[1] - width
+    outs = [pltpu.make_async_copy(
+        src, y_hbm.at[pl.ds(pl.multiple_of(row * hr, hr), hr), pl.ds(first, width)], sem.at[i])
+        for i, (src, row) in enumerate(((mine, core), (other, 1 - core)))]
+    for c in outs:
+        c.start()
+    for c in outs:
+        c.wait()
+
+
 def solution(mesh):
     def local(x, w):
         rows, depth = x.shape
         cols = w.shape[1]
         nb, nu, hr = depth // BK, cols // NC, rows // 2
-        dma = pltpu.SemaphoreType.DMA
-        r = pl.pallas_call(
+        dma, hbm = pltpu.SemaphoreType.DMA, pl.BlockSpec(memory_space=pl.ANY)
+        r, c = pl.pallas_call(
             functools.partial(kernel, nb, nu, hr),
-            out_shape=jax.ShapeDtypeStruct((rows, cols), BF16),
-            in_specs=[pl.BlockSpec(memory_space=pl.ANY)] * 2,
-            out_specs=pl.BlockSpec(memory_space=pl.ANY),
+            out_shape=[jax.ShapeDtypeStruct((rows, cols), BF16), jax.ShapeDtypeStruct((hr, 2 * NC), BF16)],
+            in_specs=[hbm] * 2,
+            out_specs=[hbm] * 2,
             scratch_shapes=[
                 pltpu.VMEM((rows, depth), BF16),
                 pltpu.VMEM((WS, depth, NC), BF16),
                 pltpu.VMEM((2, rows, NC), F32),
-                pltpu.VMEM((2, hr, NC), BF16),
+                pltpu.VMEM((4, hr, NC), BF16),
                 pltpu.VMEM((4, hr, NC), BF16),
                 pltpu.VMEM((SLOTS, hr, NC), BF16),
                 pltpu.VMEM((SLOTS, hr, NC), BF16),
                 pltpu.VMEM((2, hr, NC), BF16),
                 dma((nb,)), dma((2, nb)), dma((WS,)),
-                dma((2,)), dma((4,)),
+                dma((4,)), dma((4,)),
                 dma((SLOTS,)), dma((SLOTS,)),
-                dma((2,)), dma(()), dma((2,)),
+                dma((2,)), dma(()), dma((2,)), dma((2,)),
             ],
             compiler_params=pltpu.CompilerParams(
                 collective_id=0, has_side_effects=True, vmem_limit_bytes=63 * 1024 * 1024),
@@ -234,15 +254,28 @@
             name="rowparallel",
         )(x, w)
 
-        return pl.pallas_call(
-            last_copy,
+        across = lax.ppermute(c, "tp", [(i, (i + 2) % 4) for i in range(4)])
+        done = cols - 2 * NC
+        y = pl.pallas_call(
+            functools.partial(last_copy, done),
             out_shape=jax.ShapeDtypeStruct((rows, cols), BF16),
-            in_specs=[pl.BlockSpec(memory_space=pl.ANY)],
-            out_specs=pl.BlockSpec(memory_space=pl.ANY),
-            scratch_shapes=[pltpu.VMEM((rows // CP, CP, cols), BF16), dma((rows // CP,)), dma((rows // CP,))],
+            in_specs=[hbm], out_specs=hbm,
+            scratch_shapes=[pltpu.VMEM((rows // CP, CP, done), BF16), dma((rows // CP,)), dma((rows // CP,))],
             compiler_params=pltpu.CompilerParams(vmem_limit_bytes=63 * 1024 * 1024),
+            cost_estimate=pl.CostEstimate(flops=0, transcendentals=0, bytes_accessed=4 * rows * done),
             name="lastcopy",
         )(r)
+        across, y = lax.optimization_barrier((across, y))
+        mine = c + across
+        other = lax.ppermute(mine, "tp", [(0, 1), (1, 0), (2, 3), (3, 2)])
+        return pl.pallas_call(
+            last_units,
+            out_shape=jax.ShapeDtypeStruct((rows, cols), BF16),
+            in_specs=[hbm] + [pl.BlockSpec(memory_space=pltpu.VMEM)] * 2, out_specs=hbm,
+            input_output_aliases={0: 0},
+            scratch_shapes=[dma((2,))],
+            name="lastunits",
+        )(y, mine, other)
 
     return jax.shard_map(local, mesh=mesh, in_specs=(P("data", "tp"), P("tp", None)),
                          out_specs=P("data", None), check_vma=False)

time: 363 us -> 357 us (0.983)
  Pallas kernels: 363 us -> 352 us
    pallas_call x2 -> x3, Pallas kernels: 363 us -> 352 us  [the longest x1 334 us: local(): pl.pallas_call(functools.partial(kernel, nb, nu, hr), out_shape=[jax.Shap...]
  transfers between devices with their start and end apart: 0 -> 2, of which waited for: 0 -> 1; matrix products, arithmetic and copies ran while one was open for 0% -> 0% of each run, Pallas kernels for 0% -> 5%
where the time goes in v4:
time: 357 us; the launch traced here: 356 us
  Pallas kernels  352 us (99%)
    pallas_call x1, Pallas kernels, local(): pl.pallas_call(functools.partial(kernel, nb, nu, hr), out_shape=[jax.Shap...  334 us
    pallas_call x1, Pallas kernels, local(): pl.pallas_call(functools.partial(last_copy, done), out_shape=jax.ShapeDty...  16.5 us
  transfers between devices with their start and end apart: 2, of which 1 were waited for; matrix products, arithmetic and copies ran while one was open for 0% of the time, Pallas kernels for 5%

profile of v4, /device:TPU:0, one launch (start us, length us, event | category | flops | bytes accessed | tf_op | source)
XLA Modules:
  0.0 356.5 jit_solution(4026915806647804271)
XLA Ops:
  0.0 333.6 %rowparallel.1 = (bf16[1024,12288]{1,0:T(8,128)(2,1)}, bf16[512,512]{1,0:T(8,128)(2,1)}) custom-call(bf16[1024,12288]{1,0:T(8,128)(2,1)} %x_hbm.1, bf16[12288,12288]{1,0:T(8,128)(2,1)} %w_hbm.1), custom_call_target="tpu_custom_call" | custom-call | flops 309237645312 | bytes 352321536 | tf_op jit(solution)/shard_map/rowparallel/pallas_call | solution.py:230
  333.6 0.0 collective-permute-start
  333.7 0.0 copy-start.2
  333.7 16.5 %lastcopy.1.y_in = bf16[1024,12288]{1,0:T(8,128)(2,1)} custom-call(bf16[1024,12288]{1,0:T(8,128)(2,1)} %get-tuple-element.10.r_hbm), custom_call_target="tpu_custom_call" | custom-call | bytes 48234496 | tf_op jit(solution)/shard_map/lastcopy/pallas_call | solution.py:259
  350.2 0.0 collective-permute-done
  350.2 0.0 copy-done.2
  350.2 1.2 add.3.mine
  351.4 0.0 copy-start
  351.4 0.3 collective-permute-start.1
  351.7 1.6 collective-permute-done.1.other
  353.3 0.0 copy-done
  353.3 0.0 copy-start.1
  353.3 0.8 copy-done.1
  354.1 2.2 lastunits.1
Async XLA Ops:
  333.6 16.6 %collective-permute-start = (bf16[512,512]{1,0:T(8,128)(2,1)}, bf16[512,512]{1,0:T(8,128)(2,1)}, u32[]{:S(2)}, u32[]{:S(2)}) collective-permute-start(bf16[512,512]{1,0:T(8,128)(2,1)} %get-tuple-element.9), channel_id=1, source_target_pairs={{0,2},{1,3},{2,0},{3,1},{4,6},{5,7},{6,4},{7,5}} | collective-permute-start | bytes 1572872 | tf_op jit(solution)/shard_map/ppermute | solution.py:257
  333.7 16.5 %copy-start.2 = (bf16[512,512]{1,0:T(8,128)(2,1)S(1)}, bf16[512,512]{1,0:T(8,128)(2,1)}, u32[]{:S(2)}) copy-start(bf16[512,512]{1,0:T(8,128)(2,1)} %get-tuple-element.9) | copy-start | bytes 1572868
  351.4 1.9 copy-start
  351.4 1.9 collective-permute-start.1
  353.3 0.8 copy-start.1
